TPU v7x, 32 devices: a whole 2x2x4 slice. The times are simulated.
32 devices in a mesh: grp: 4 (over x, core), tile: 8 (over z, y).
Axes of the slice: x: 2, y: 2, z: 4, core: 2. Of those that a mesh axis runs over, the one named last changes fastest.
Arguments:
- start_block: float32 [65536, 256], P(('grp', 'tile')), may hold values from -8 to 8
- dense_tiles: float32 [32, 2048, 2048], P(('grp', 'tile')), as said below
- basis: float32 [32, 48, 2048], P(('grp', 'tile')), may hold values from -0.125 to 0.125
- coupling: float32 [4, 8, 48, 1536], P(None, 'tile', None, 'grp'), as said below
- admissible: int32 [4, 8, 32], P(None, 'tile', 'grp'), may hold values from 0 to 1, as said below
Outputs:
- modes: float32 [65536, 256], P(('grp', 'tile'))
Inputs may be any that keep to these rules, and one draw needn't show every extreme that they name: admissible is symmetric over tile pairs (the entry for row tile i and column tile j equals that for row tile j and column tile i) and 0 where the row tile equals the column tile. `dense_tiles`: each dense tile is symmetric: a positive scale times a diagonal plus an unstructured symmetric off-diagonal part. The coupling, read as a matrix of order 32 * 48, is symmetric: block S_ji is the transpose of S_ij.
All inputs are finite; a program needn't handle non-finite values.
Results may differ from a plain program's by a relative error of at most 0.0003.
Values sent between devices are 32-bit elements; how exact they have to be, the bound alone decides.
No kernel may reach another device: no remote copies, remote signals or barrier semaphores. Data moves between devices by JAX's collectives and lax.ppermute only.
A program may use at most 128 MiB of HBM per device.

v0:
```python
import jax
import jax.numpy as jnp
from jax import lax
from jax.sharding import PartitionSpec as P


def body(start_block, dense_tiles, basis, coupling, admissible):
    hp = lax.Precision.HIGHEST
    groups = coupling.shape[0]
    width = basis.shape[1]
    span = coupling.shape[3] // width
    modes_count = start_block.shape[1]
    flags = admissible.astype(jnp.float32).reshape(groups, 1, span, 1)
    masked = (coupling.reshape(groups, width, span, width) * flags).reshape(
        groups * width, span * width
    )
    dense = dense_tiles[0]
    rows_basis = basis[0]
    total_rows = lax.axis_size("grp") * lax.axis_size("tile") * start_block.shape[0]

    def add_columns(piece):
        return jnp.dot(masked, piece, precision=hp, preferred_element_type=jnp.float32)

    def apply_operator(field):
        coeffs = jnp.dot(rows_basis, field, precision=hp)
        partial_rows = add_columns(lax.all_gather(coeffs, "tile", axis=0, tiled=True))
        summed = lax.psum_scatter(
            partial_rows.reshape(groups, width, modes_count), "grp", scatter_dimension=0, tiled=True
        )[0]
        far = lax.dot_general(rows_basis, summed, (((0,), (0,)), ((), ())), precision=hp)
        near = jnp.dot(dense, field, precision=hp)
        return far + near

    def whitening(field):
        local_gram = lax.dot_general(field, field, (((0,), (0,)), ((), ())), precision=hp)
        gram = lax.psum(local_gram, ("grp", "tile")) / jnp.float32(total_rows)
        lower = jnp.linalg.cholesky(gram)
        return lax.linalg.triangular_solve(
            lower, jnp.eye(modes_count, dtype=gram.dtype), left_side=True, lower=True
        )

    image = apply_operator(start_block)
    inverse = whitening(image)
    further = apply_operator(image)
    image = jnp.dot(further, inverse.T, precision=hp)
    inverse = whitening(image)
    return jnp.dot(image, inverse.T, precision=hp)


def solution(mesh):
    placed = (
        P(("grp", "tile"), None),
        P(("grp", "tile"), None, None),
        P(("grp", "tile"), None, None),
        P(None, "tile", None, "grp"),
        P(None, "tile", "grp"),
    )
    return jax.shard_map(
        body, mesh=mesh, in_specs=placed, out_specs=P(("grp", "tile"), None), check_vma=False
    )
```

profile of v0, /device:TPU:0, one launch (start us, length us, event | category | flops | bytes accessed | tf_op | source)
XLA Modules:
  0.0 498.3 jit_solution(8622387900580312000)
XLA Ops:
  6.5 0.8 convert_element_type.9
  7.4 0.1 mul.18
  7.4 0.1 mul.19
  7.5 0.6 copy-done
  8.1 2.1 fusion.19
  10.3 32.8 %all_gather.6 = f32[384,256]{1,0:T(8,128)S(1)} all-gather(f32[48,256]{1,0:T(8,128)S(1)} %fusion.19), channel_id=1, replica_groups=mesh['grp'=4,'tile'=8] {'tile'}, dimensions={0}, use_global_device_ids=true | all-gather | bytes 442368 | tf_op jit(solution)/shard_map/all_gather | solution.py:26
  43.0 1.2 fusion.14
  44.2 0.0 all-reduce.4.cloned.1.call-start
  44.3 18.6 %fusion.2 = f32[2048,256]{0,1:T(8,128)} fusion(f32[2048,256]{1,0:T(8,128)S(1)} %copy-done, f32[1,2048,2048]{2,1,0:T(8,128)} %param.9), kind=kOutput, calls=%fused_computation.6 | convolution fusion | flops 12884901888 | bytes 20971520 | tf_op jit(solution)/shard_map/dot_general | solution.py:31
  62.9 2.4 reduce-scatter.3.cloned.1.call-done
  65.3 2.8 convolution_bitcast_fusion
  68.1 1.3 copy-done.3
  69.4 2.7 fusion.4
  72.1 4.3 fusion.9
  76.5 18.3 %fusion = f32[256,2048]{1,0:T(8,128)} fusion(f32[1,2048,2048]{2,1,0:T(8,128)} %param.9, f32[2048,256]{0,1:T(8,128)S(1)} %copy-done.4, f32[2048,256]{0,1:T(8,128)S(1)} %copy-done.2), kind=kOutput, calls=%fused_computation.4 | convolution fusion | flops 12885426176 | bytes 23068672 | tf_op jit(solution)/shard_map/dot_general | solution.py:31
  94.8 0.0 reduce-scatter.5.cloned.1.call-start
  94.9 31.3 %all_gather.7 = f32[384,256]{1,0:T(8,128)S(1)} all-gather(f32[48,256]{1,0:T(8,128)S(1)} %fusion.9), channel_id=1, replica_groups=mesh['grp'=4,'tile'=8] {'tile'}, dimensions={0}, use_global_device_ids=true | all-gather | bytes 442368 | tf_op jit(solution)/shard_map/all_gather | solution.py:26
  126.2 1.2 fusion.12
  127.4 0.0 all-reduce.6.cloned.1.call-start
  127.5 94.4 %all-reduce.4.cloned.1.call-done = f32[256,256]{0,1:T(8,128)} async-done(((f32[256,256]{0,1:T(8,128)}), f32[256,256]{0,1:T(8,128)}) %all-reduce.4.cloned.1.call-update) | async-done | bytes 262160 | tf_op jit(solution)/shard_map/psum | solution.py:36
  221.9 1.0 broadcast_multiply_fusion.1
  222.9 0.1 copy.8
  223.0 1.0 fusion.30
  224.0 11.7 %cholesky.130 = f32[128,128]{1,0:T(8,128)S(1)} custom-call(f32[128,128]{1,0:T(8,128)S(1)} %cholesky.194), custom_call_target="Cholesky" | custom-call | tf_op jit(solution)/shard_map/jit(cholesky)/cholesky | solution.py:37
  235.8 9.8 %custom-call.13 = f32[1,128,128]{1,2,0:T(8,128)S(1)} custom-call(f32[1,128,128]{2,1,0:T(8,128)S(1)} %get-tuple-element.50), custom_call_target="InvertDiagBlocksLowerTriangular" | custom-call | tf_op jit(solution)/shard_map/jit(cholesky)/cholesky | solution.py:37
  245.6 0.2 constant_dynamic-update-slice_fusion.3
  245.8 0.3 convolution_subtract_fusion.3
  246.1 11.7 %cholesky.147 = f32[128,128]{1,0:T(8,128)S(1)} custom-call(f32[128,128]{1,0:T(8,128)S(1)} %convolution_subtract_fusion.3), custom_call_target="Cholesky" | custom-call | tf_op jit(solution)/shard_map/jit(cholesky)/cholesky | solution.py:37
  257.8 0.7 compare_reduce_fusion.2
  259.9 0.1 broadcast.100
  259.9 4.1 while.4
  260.0 0.7 fusion.71
  260.6 1.3 bitcast_dynamic-update-slice_fusion.4
  262.0 0.7 fusion.71
  262.7 1.3 bitcast_dynamic-update-slice_fusion.4
  264.0 20.1 %custom-call.14 = f32[2,128,128]{1,2,0:T(8,128)S(1)} custom-call(f32[2,128,128]{2,1,0:T(8,128)S(1)} %get-tuple-element.21), custom_call_target="InvertDiagBlocksLowerTriangular" | custom-call | tf_op jit(solution)/shard_map/triangular_solve/custom-call.0 | solution.py:38
  284.1 0.3 fusion.36
  284.4 0.3 convolution_subtract_fusion.1
  284.7 0.3 fusion.43
  285.0 3.5 convolution_add_fusion
  288.6 3.6 fusion.21
  292.2 1.3 copy-done.5
  293.5 4.3 fusion.54
  297.8 125.8 %all-reduce.6.cloned.1.call-done = f32[256,256]{0,1:T(8,128)} async-done(((f32[256,256]{0,1:T(8,128)}), f32[256,256]{0,1:T(8,128)}) %all-reduce.6.cloned.1.call-update) | async-done | bytes 262160 | tf_op jit(solution)/shard_map/psum | solution.py:36
  423.6 1.0 broadcast_multiply_fusion
  424.6 0.1 copy.10
  424.7 1.0 fusion.29
  425.7 11.9 %cholesky.164 = f32[128,128]{1,0:T(8,128)S(1)} custom-call(f32[128,128]{1,0:T(8,128)S(1)} %cholesky.197), custom_call_target="Cholesky" | custom-call | tf_op jit(solution)/shard_map/jit(cholesky)/cholesky | solution.py:37
  437.6 9.8 %custom-call.15 = f32[1,128,128]{1,2,0:T(8,128)S(1)} custom-call(f32[1,128,128]{2,1,0:T(8,128)S(1)} %get-tuple-element.46), custom_call_target="InvertDiagBlocksLowerTriangular" | custom-call | tf_op jit(solution)/shard_map/jit(cholesky)/cholesky | solution.py:37
  447.5 0.2 constant_dynamic-update-slice_fusion.1
  447.7 0.3 convolution_subtract_fusion.2
  447.9 11.7 %cholesky.181 = f32[128,128]{1,0:T(8,128)S(1)} custom-call(f32[128,128]{1,0:T(8,128)S(1)} %convolution_subtract_fusion.2), custom_call_target="Cholesky" | custom-call | tf_op jit(solution)/shard_map/jit(cholesky)/cholesky | solution.py:37
  459.7 0.6 compare_reduce_fusion
  460.3 0.6 compare_reduce_fusion.1
  462.3 3.9 while.5
  462.3 0.6 fusion.72
  462.9 1.4 bitcast_dynamic-update-slice_fusion.5
  464.3 0.6 fusion.72
  464.9 1.4 bitcast_dynamic-update-slice_fusion.5
  466.2 19.7 %custom-call.16 = f32[2,128,128]{1,2,0:T(8,128)S(1)} custom-call(f32[2,128,128]{2,1,0:T(8,128)S(1)} %get-tuple-element.22), custom_call_target="InvertDiagBlocksLowerTriangular" | custom-call | tf_op jit(solution)/shard_map/triangular_solve/custom-call.0 | solution.py:38
  485.9 0.3 fusion.34
  486.2 0.3 convolution_subtract_fusion
  486.5 0.3 fusion.39
  486.8 4.7 fusion.25
  (37 shorter events, 0.4 us)
Async XLA Ops:
  6.5 1.6 copy-start
  6.5 36.5 %copy-start.7 = (f32[4,1,48,384]{3,2,1,0:T(8,128)S(1)}, f32[4,1,48,384]{3,2,1,0:T(8,128)}, u32[]{:S(2)}) copy-start(f32[4,1,48,384]{3,2,1,0:T(8,128)} %param.11) | copy-start | bytes 884740
  6.5 58.7 %reduce-scatter.3.cloned.1.call-start = ((), (), s32[]{:S(2)}) async-start(), calls=%async_computation.2 | async-start | bytes 245760 | tf_op jit(solution)/shard_map/reduce_scatter | solution.py:27
  44.2 21.0 %copy-start.6 = (f32[1,48,2048]{2,1,0:T(8,128)S(1)}, f32[1,48,2048]{2,1,0:T(8,128)}, u32[]{:S(2)}) copy-start(f32[1,48,2048]{2,1,0:T(8,128)} %param.10) | copy-start | bytes 1179652
  44.2 177.7 %all-reduce.4.cloned.1.call-start = ((), (), s32[]{:S(2)}) async-start(), calls=%async_computation.4 | async-start | bytes 524288 | tf_op jit(solution)/shard_map/psum | solution.py:36
  65.3 4.1 copy-start.1
  68.1 1.3 copy-start.3
  72.1 4.3 copy-start.2
  72.1 4.4 copy-start.4
  94.8 190.2 %reduce-scatter.5.cloned.1.call-start = ((), (), s32[]{:S(2)}) async-start(), calls=%async_computation.3 | async-start | bytes 245760 | tf_op jit(solution)/shard_map/reduce_scatter | solution.py:27
  127.4 296.2 %all-reduce.6.cloned.1.call-start = ((), (), s32[]{:S(2)}) async-start(), calls=%async_computation.5 | async-start | bytes 524288 | tf_op jit(solution)/shard_map/psum | solution.py:36
  292.1 1.4 copy-start.5
Sparse Core Ops, SparseCore 0:
  44.4 20.8 reduce-scatter.2
  95.0 126.9 all-reduce.3
  224.4 18.9 reduce-scatter.4
  298.0 125.6 all-reduce.5
where the time goes:
time: 506 us; the launch traced here: 498 us
  waiting for transfers between devices  223 us (44%)
  other arithmetic  113 us (22%)
  matrix products  70.1 us (14%)
  blocking collectives  64.1 us (13%)
  between operations  16.1 us (3%)
  local copies, waits for them, and re-layouts  11.8 us (2%)
    psum x2, waiting for transfers between devices, whitening(): gram = lax.psum(local_gram, ('grp', 'tile')) / jnp.float32(total_rows)  220 us
    another operation x13, other arithmetic, whitening(): lower = jnp.linalg.cholesky(gram)  68.8 us
    all_gather x2, blocking collectives, apply_operator(): lax.all_gather(coeffs, 'tile', axis=0, tiled=True)  64.1 us
    another operation x5, other arithmetic, whitening(): lax.linalg.triangular_solve(lower, jnp.eye(modes_count, dtype=gram.dtype)...  39.8 us
    dot_general x2, matrix products, apply_operator(): near = jnp.dot(dense, field, precision=hp)  36.9 us
  transfers between devices with their start and end apart: 4, of which 3 were waited for; matrix products, arithmetic and copies ran while one was open for 16% of the time, Pallas kernels for 0%

commit v1 on v0

--- a/solution.py
+++ b/solution.py
@@ -1,7 +1,15 @@
+import functools
 import jax
 import jax.numpy as jnp
 from jax import lax
 from jax.sharding import PartitionSpec as P
+
+
+def supply_all_patches(chunk, ax_name):
+    return lax.all_gather(chunk, axis_name=ax_name).sum(axis=0)
+
+
+solve_bench_for = functools.partial(supply_all_patches, ax_name=("grp", "tile"))
 
 
 def body(start_block, dense_tiles, basis, coupling, admissible):
@@ -33,7 +41,7 @@
 
     def whitening(field):
         local_gram = lax.dot_general(field, field, (((0,), (0,)), ((), ())), precision=hp)
-        gram = lax.psum(local_gram, ("grp", "tile")) / jnp.float32(total_rows)
+        gram = solve_bench_for(local_gram) / jnp.float32(total_rows)
         lower = jnp.linalg.cholesky(gram)
         return lax.linalg.triangular_solve(
             lower, jnp.eye(modes_count, dtype=gram.dtype), left_side=True, lower=True

time: 506 us -> 450 us (0.89)
  waiting for transfers between devices: 223 us -> 147 us
  other arithmetic: 113 us -> 127 us
    psum x2 -> x0, waiting for transfers between devices: 220 us -> none  [whitening(): gram = lax.psum(local_gram, ('grp', 'tile')) / jnp.float32(total_rows)]
    all_gather x0 -> x2, waiting for transfers between devices: none -> 145 us  [supply_all_patches(): return lax.all_gather(chunk, axis_name=ax_name).sum(axis=0)]
    another operation x13, other arithmetic: 68.8 us -> 79.2 us  [whitening(): lower = jnp.linalg.cholesky(gram)]
    reduce_sum x0 -> x2, other arithmetic: none -> 7.86 us  [supply_all_patches(): return lax.all_gather(chunk, axis_name=ax_name).sum(axis=0)]
  transfers between devices with their start and end apart: 4 -> 4, of which waited for: 3 -> 3; matrix products, arithmetic and copies ran while one was open for 16% -> 11% of each run, Pallas kernels for 0% -> 0%
where the time goes in v1:
time: 450 us; the launch traced here: 442 us
  waiting for transfers between devices  147 us (33%)
  other arithmetic  127 us (28%)
  matrix products  75.1 us (17%)
  blocking collectives  64 us (14%)
  between operations  16.4 us (4%)
  local copies, waits for them, and re-layouts  11.8 us (3%)
    all_gather x2, waiting for transfers between devices, supply_all_patches(): return lax.all_gather(chunk, axis_name=ax_name).sum(axis=0)  145 us
    another operation x13, other arithmetic, whitening(): lower = jnp.linalg.cholesky(gram)  79.2 us
    all_gather x2, blocking collectives, apply_operator(): lax.all_gather(coeffs, 'tile', axis=0, tiled=True)  64 us
    another operation x5, other arithmetic, whitening(): lax.linalg.triangular_solve(lower, jnp.eye(modes_count, dtype=gram.dtype)...  39.4 us
    dot_general x2, matrix products, apply_operator(): near = jnp.dot(dense, field, precision=hp)  37.9 us
    dot_general x2, matrix products, whitening(): lax.dot_general(field, field, (((0,), (0,)), ((), ())), precision=hp)  10.6 us
  transfers between devices with their start and end apart: 4, of which 3 were waited for; matrix products, arithmetic and copies ran while one was open for 11% of the time, Pallas kernels for 0%

profile of v1, /device:TPU:0, one launch (start us, length us, event | category | flops | bytes accessed | tf_op | source)
XLA Modules:
  0.0 441.8 jit_solution(3478250483609635464)
XLA Ops:
  6.5 1.6 copy-done
  8.1 2.1 fusion.19
  10.2 32.8 %all_gather.18 = f32[384,256]{1,0:T(8,128)S(1)} all-gather(f32[48,256]{1,0:T(8,128)S(1)} %fusion.19), channel_id=1, replica_groups=mesh['grp'=4,'tile'=8] {'tile'}, dimensions={0}, use_global_device_ids=true | all-gather | bytes 442368 | tf_op jit(solution)/shard_map/all_gather | solution.py:34
  43.0 0.1 mul.18
  43.1 0.1 mul.19
  43.2 1.2 fusion.14
  44.4 0.0 reduce-scatter.5.cloned.1.call-start
  44.4 18.6 %fusion.2 = f32[2048,256]{0,1:T(8,128)} fusion(f32[2048,256]{1,0:T(8,128)S(1)} %copy-done, f32[1,2048,2048]{2,1,0:T(8,128)} %param.9), kind=kOutput, calls=%fused_computation.6 | convolution fusion | flops 12884901888 | bytes 20971520 | tf_op jit(solution)/shard_map/dot_general | solution.py:39
  63.0 2.4 reduce-scatter.3.cloned.1.call-done
  65.4 2.8 convolution_bitcast_fusion
  68.2 2.0 fusion.9
  70.2 31.3 %all_gather.19 = f32[384,256]{1,0:T(8,128)S(1)} all-gather(f32[48,256]{1,0:T(8,128)S(1)} %fusion.9), channel_id=1, replica_groups=mesh['grp'=4,'tile'=8] {'tile'}, dimensions={0}, use_global_device_ids=true | all-gather | bytes 442368 | tf_op jit(solution)/shard_map/all_gather | solution.py:34
  101.4 1.2 fusion.12
  102.6 0.0 reduce-scatter.5.cloned.1.call-update
  102.6 0.0 all-gather.5.cloned.1.call-start
  102.7 6.3 %fusion.4 = f32[256,256]{1,0:T(8,128)} fusion(f32[2048,256]{0,1:T(8,128)} %copy-done.2, f32[2048,256]{0,1:T(8,128)} %fusion.2), kind=kOutput, calls=%fused_computation.8 | convolution fusion | flops 1611137024 | bytes 4456448 | tf_op jit(solution)/shard_map/dot_general | solution.py:43
  108.9 0.0 all-gather.5.cloned.1.call-update
  109.0 0.3 all-gather.7.cloned.1.call-start
  109.3 19.4 %fusion = f32[256,2048]{1,0:T(8,128)} fusion(f32[1,2048,2048]{2,1,0:T(8,128)} %param.9, f32[2048,256]{0,1:T(8,128)} %copy-done.2, f32[2048,256]{0,1:T(8,128)} %fusion.2), kind=kOutput, calls=%fused_computation.4 | convolution fusion | flops 12885426176 | bytes 23068672 | tf_op jit(solution)/shard_map/dot_general | solution.py:39
  128.7 4.8 %convolution_add_fusion = f32[256,2048]{1,0:T(8,128)} fusion(f32[256,2048]{1,0:T(8,128)} %fusion, f32[1,48,2048]{2,1,0:T(8,128)S(1)} %copy-done.4, f32[1,48,256]{2,1,0:T(8,128)} %reduce-scatter.5.cloned.1.call-done), kind=kOutput, calls=%fused_computation.13 | convolution fusion | flops 302514176 | bytes 4636672 | tf_op jit(solution)/shard_map/dot_general | solution.py:38
  133.4 69.0 %all-gather.5.cloned.1.call-done = f32[8192,256]{1,0:T(8,128)} async-done(((f32[256,256]{1,0:T(8,128)}), f32[8192,256]{1,0:T(8,128)}) %all-gather.5.cloned.1.call-update) | async-done | bytes 8388624 | tf_op jit(solution)/shard_map/all_gather | solution.py:9
  202.5 3.9 reduce_sum.18
  206.4 0.1 copy.10
  206.6 0.1 copy.11
  206.8 11.7 %cholesky.130 = f32[128,128]{1,0:T(8,128)S(1)} custom-call(f32[128,128]{1,0:T(8,128)S(1)} %cholesky.194), custom_call_target="Cholesky" | custom-call | tf_op jit(solution)/shard_map/jit(cholesky)/cholesky | solution.py:45
  218.5 9.8 %custom-call.13 = f32[1,128,128]{1,2,0:T(8,128)S(1)} custom-call(f32[1,128,128]{2,1,0:T(8,128)S(1)} %get-tuple-element.50), custom_call_target="InvertDiagBlocksLowerTriangular" | custom-call | tf_op jit(solution)/shard_map/jit(cholesky)/cholesky | solution.py:45
  228.4 0.2 constant_dynamic-update-slice_fusion.3
  228.6 0.3 convolution_subtract_fusion.3
  228.8 22.0 %cholesky.147 = f32[128,128]{1,0:T(8,128)S(1)} custom-call(f32[128,128]{1,0:T(8,128)S(1)} %convolution_subtract_fusion.3), custom_call_target="Cholesky" | custom-call | tf_op jit(solution)/shard_map/jit(cholesky)/cholesky | solution.py:45
  250.9 0.7 compare_reduce_fusion.2
  252.9 0.1 broadcast.100
  253.0 4.1 while.4
  253.0 0.7 fusion.71
  253.7 1.3 bitcast_dynamic-update-slice_fusion.4
  255.1 0.7 fusion.71
  255.7 1.3 bitcast_dynamic-update-slice_fusion.4
  257.1 19.7 %custom-call.14 = f32[2,128,128]{1,2,0:T(8,128)S(1)} custom-call(f32[2,128,128]{2,1,0:T(8,128)S(1)} %get-tuple-element.21), custom_call_target="InvertDiagBlocksLowerTriangular" | custom-call | tf_op jit(solution)/shard_map/triangular_solve/custom-call.0 | solution.py:46
  276.8 0.3 fusion.36
  277.1 0.3 convolution_subtract_fusion.1
  277.3 0.3 fusion.43
  277.7 5.2 %fusion.21 = f32[2048,256]{1,0:T(8,128)S(1)} fusion(f32[256,2048]{1,0:T(8,128)} %convolution_add_fusion, f32[128,256]{1,0:T(8,128)S(1)} %fusion.43, f32[128,256]{1,0:T(8,128)S(1)} %fusion.36), kind=kOutput, calls=%fused_computation.32 | convolution fusion | flops 1610678272 | bytes 4456448 | tf_op jit(solution)/shard_map/dot_general | solution.py:53
  282.9 1.4 copy-done.3
  284.2 4.3 fusion.54
  288.6 75.9 %all-gather.7.cloned.1.call-done = f32[8192,256]{1,0:T(8,128)} async-done(((f32[256,256]{1,0:T(8,128)}), f32[8192,256]{1,0:T(8,128)}) %all-gather.7.cloned.1.call-update) | async-done | bytes 8388624 | tf_op jit(solution)/shard_map/all_gather | solution.py:9
  364.5 3.9 reduce_sum.19
  368.4 0.1 copy.12
  368.6 0.1 copy.13
  368.8 11.9 %cholesky.164 = f32[128,128]{1,0:T(8,128)S(1)} custom-call(f32[128,128]{1,0:T(8,128)S(1)} %cholesky.197), custom_call_target="Cholesky" | custom-call | tf_op jit(solution)/shard_map/jit(cholesky)/cholesky | solution.py:45
  380.8 9.8 %custom-call.15 = f32[1,128,128]{1,2,0:T(8,128)S(1)} custom-call(f32[1,128,128]{2,1,0:T(8,128)S(1)} %get-tuple-element.46), custom_call_target="InvertDiagBlocksLowerTriangular" | custom-call | tf_op jit(solution)/shard_map/jit(cholesky)/cholesky | solution.py:45
  390.6 0.2 constant_dynamic-update-slice_fusion.1
  390.8 0.3 convolution_subtract_fusion.2
  391.0 11.7 %cholesky.181 = f32[128,128]{1,0:T(8,128)S(1)} custom-call(f32[128,128]{1,0:T(8,128)S(1)} %convolution_subtract_fusion.2), custom_call_target="Cholesky" | custom-call | tf_op jit(solution)/shard_map/jit(cholesky)/cholesky | solution.py:45
  402.8 0.6 compare_reduce_fusion.1
  403.4 0.7 compare_reduce_fusion
  405.5 4.1 while.5
  405.5 0.6 fusion.72
  406.1 1.4 bitcast_dynamic-update-slice_fusion.5
  407.6 0.6 fusion.72
  408.1 1.4 bitcast_dynamic-update-slice_fusion.5
  409.6 19.7 %custom-call.16 = f32[2,128,128]{1,2,0:T(8,128)S(1)} custom-call(f32[2,128,128]{2,1,0:T(8,128)S(1)} %get-tuple-element.22), custom_call_target="InvertDiagBlocksLowerTriangular" | custom-call | tf_op jit(solution)/shard_map/triangular_solve/custom-call.0 | solution.py:46
  429.3 0.3 fusion.34
  429.6 0.3 convolution_subtract_fusion
  429.8 0.3 fusion.39
  430.2 4.7 %fusion.25 = f32[2048,256]{1,0:T(8,128)} fusion(f32[2048,256]{1,0:T(8,128)} %copy-done.3, f32[128,256]{1,0:T(8,128)S(1)} %fusion.39, f32[128,256]{1,0:T(8,128)S(1)} %fusion.34), kind=kOutput, calls=%fused_computation.36 | convolution fusion | flops 1610678272 | bytes 4456448 | tf_op jit(solution)/shard_map/dot_general | solution.py:55
  (39 shorter events, 0.5 us)
Async XLA Ops:
  6.5 1.6 copy-start
  6.5 36.5 %copy-start.6 = (s32[4,1,8]{2,1,0:T(1,128)S(1)}, s32[4,1,8]{2,1,0:T(1,128)}, u32[]{:S(2)}) copy-start(s32[4,1,8]{2,1,0:T(1,128)} %param.12) | copy-start | bytes 388
  6.5 36.6 %copy-start.5 = (f32[4,1,48,384]{3,2,1,0:T(8,128)S(1)}, f32[4,1,48,384]{3,2,1,0:T(8,128)}, u32[]{:S(2)}) copy-start(f32[4,1,48,384]{3,2,1,0:T(8,128)} %param.11) | copy-start | bytes 884740
  6.5 58.8 %reduce-scatter.3.cloned.1.call-start = ((), (), s32[]{:S(2)}) async-start(), calls=%async_computation.2 | async-start | bytes 245760 | tf_op jit(solution)/shard_map/reduce_scatter | solution.py:35
  44.4 21.0 %copy-start.4 = (f32[1,48,2048]{2,1,0:T(8,128)S(1)}, f32[1,48,2048]{2,1,0:T(8,128)}, u32[]{:S(2)}) copy-start(f32[1,48,2048]{2,1,0:T(8,128)} %param.10) | copy-start | bytes 1179652
  44.4 84.3 %reduce-scatter.5.cloned.1.call-start = ((), (), s32[]{:S(2)}) async-start(), calls=%async_computation.3 | async-start | bytes 245760 | tf_op jit(solution)/shard_map/reduce_scatter | solution.py:35
  65.4 2.8 copy-start.1
  68.2 2.0 copy-start.2
  102.6 99.8 %all-gather.5.cloned.1.call-start = ((), (), s32[]{:S(2)}) async-start(), calls=%async_computation.4 | async-start | bytes 8650752 | tf_op jit(solution)/shard_map/all_gather | solution.py:9
  109.0 255.5 %all-gather.7.cloned.1.call-start = ((), (), s32[]{:S(2)}) async-start(), calls=%async_computation.5 | async-start | bytes 8650752 | tf_op jit(solution)/shard_map/all_gather | solution.py:9
  282.8 1.4 copy-start.3
Sparse Core Ops, SparseCore 0:
  44.5 20.8 reduce-scatter.2
  102.8 19.5 reduce-scatter.4
  125.4 77.0 all-gather.4
  288.7 75.7 all-gather.6
